TPU v7x, 128 devices: a whole 4x4x4 slice. The times are simulated.
128 devices in a mesh: col: 8 (over x, z_lo), row: 16 (over y, z_hi, core).
Axes of the slice: x: 4, y: 4, z: 4 (z_hi: 2, z_lo: 2; z = z_hi * 2 + z_lo), core: 2. Of those that a mesh axis runs over, the one named last changes fastest.
Arguments:
- data: bfloat16 [32768, 8192], P('row', 'col'), may hold values from -6 to 6
- column_scale: float32 [8192], P('col'), may hold values from 0.25 to 4
- keep_mask: int32 [32768, 8192], P('row', 'col'), may hold values 0 or 1
Outputs:
- band: float32 [8192, 5, 1024], P('col', None, 'row')
All inputs are finite; a program needn't handle non-finite values. No bound on the sum of `keep_mask` on one device may be relied on, other than what follows from the above.
Results may differ from a plain program's by a relative error of at most 0.0012.
Values may be sent and summed in bfloat16 or wider, within the bound.
A program may use at most 128 MiB of HBM per device.

v0:
```python
import jax
import jax.numpy as jnp
from jax import lax
from jax.sharding import Mesh
from jax.sharding import PartitionSpec as P

ROW = ("row_0", "row_1", "row_2")


def copy_for_each(value, axis):
    peers = lax.axis_size(axis)
    return lax.all_to_all(
        jnp.broadcast_to(value[None], (peers, *value.shape)), axis, 0, 0, tiled=True
    )


def of_everyone(value, axis):
    return copy_for_each(value, axis).sum(axis=0)


def passed_along(block, axis, distance):
    devices = range(lax.axis_size(axis))
    route = [((i - distance) % len(devices), i) for i in devices]
    return lax.ppermute(block, axis, route)


def split_up(value, dim, peers):
    dims = value.shape
    tiles = value.reshape(*dims[:dim], peers, dims[dim] // peers, *dims[dim + 1 :])
    return jnp.moveaxis(tiles, dim, 0)


def scatter_pairs(value, chips, core, dim):
    sizes = (lax.axis_size(chips), lax.axis_size(core))
    tiles = split_up(value, dim, sizes[0] * sizes[1])
    inside = tiles.shape[1:]
    tiles = tiles.reshape(*sizes, *inside).swapaxes(0, 1).reshape(-1, *inside)
    tiles = lax.psum_scatter(tiles, core, scatter_dimension=0, tiled=True)
    return lax.psum_scatter(tiles, chips, scatter_dimension=0, tiled=True)[0]


def product(left, right):
    return lax.dot_general(
        left, right, (((0,), (0,)), ((), ())), preferred_element_type=jnp.float32
    )


def on_device(data, column_scale, keep_mask):
    values = data.astype(jnp.float32) * column_scale[None, :]
    colsq = of_everyone(jnp.sum(values * values, axis=0), ROW)
    total_rows = data.shape[0] * lax.axis_size(ROW)
    divisor = jnp.minimum(jnp.sqrt(colsq + 1.0), jnp.sqrt(jnp.float32(total_rows)))
    scaled = (keep_mask.astype(jnp.float32) * values / divisor[None, :]).astype(jnp.bfloat16)
    offsets = lax.axis_size("col") // 2 + 1
    panels = [scaled]
    current = scaled
    for offset in range(1, offsets):
        current = passed_along(current, "col", -1)
        panels.append(current)
    terms = jnp.stack([product(scaled, other) for other in panels], axis=1)
    return scatter_pairs(terms, ("row_0", "row_1"), "row_2", 2)


def solution(mesh):
    split = Mesh(
        mesh.devices.reshape(mesh.shape["col"], 4, 2, 2), ("col", "row_0", "row_1", "row_2")
    )
    return jax.shard_map(
        on_device,
        mesh=split,
        in_specs=(P(ROW, "col"), P("col"), P(ROW, "col")),
        out_specs=P("col", None, ROW),
        check_vma=False,
    )
```

profile of v0, /device:TPU:0, one launch (start us, length us, event | category | flops | bytes accessed | tf_op | source)
XLA Modules:
  0.0 592.7 jit_solution(15488306527559406014)
XLA Ops:
  6.5 0.0 reduce-scatter.3.cloned.1.call-start
  6.5 3.3 multiply_reduce_fusion
  9.9 15.5 %all_to_all.6 = f32[16,1,1024]{2,1,0:T(1,128)S(1)} all-to-all(f32[16,1,1024]{2,1,0:T(1,128)S(1)} %broadcast_in_dim.2), channel_id=1, replica_groups=mesh['col'=8,'row_0'=4,'row_1'=2,'row_2'=2] {'row_0','row_1','row_2'}, dimensions={0} | all-to-all | bytes 131072 | tf_op jit(solution)/shard_map/all_to_all | solution.py:12
  25.4 0.1 reduce_sum.19
  25.5 0.0 copy-done
  25.5 5.5 divide_convert_fusion
  31.0 3.3 collective-permute-start
  34.2 90.1 %collective-permute-done = bf16[2048,1024]{1,0:T(8,128)(2,1)S(1)} collective-permute-done((bf16[2048,1024]{1,0:T(8,128)(2,1)S(1)}, bf16[2048,1024]{1,0:T(8,128)(2,1)S(1)}, u32[]{:S(2)}, u32[]{:S(2)}) %collective-permute-start) | collective-permute-done | bytes 4194336 | tf_op jit(solution)/shard_map/ppermute | solution.py:24
  124.4 4.6 collective-permute-start.1
  128.9 89.3 %collective-permute-done.1 = bf16[2048,1024]{1,0:T(8,128)(2,1)S(1)} collective-permute-done((bf16[2048,1024]{1,0:T(8,128)(2,1)S(1)}, bf16[2048,1024]{1,0:T(8,128)(2,1)S(1)}, u32[]{:S(2)}, u32[]{:S(2)}) %collective-permute-start.1) | collective-permute-done | bytes 4194336 | tf_op jit(solution)/shard_map/ppermute | solution.py:24
  218.2 4.6 collective-permute-start.2
  222.8 88.4 %collective-permute-done.2 = bf16[2048,1024]{1,0:T(8,128)(2,1)} collective-permute-done((bf16[2048,1024]{1,0:T(8,128)(2,1)S(1)}, bf16[2048,1024]{1,0:T(8,128)(2,1)}, u32[]{:S(2)}, u32[]{:S(2)}) %collective-permute-start.2) | collective-permute-done | bytes 4194336 | tf_op jit(solution)/shard_map/ppermute | solution.py:24
  311.2 0.0 copy-done.1
  311.2 4.7 collective-permute-start.3
  315.9 4.8 fusion
  320.7 0.6 constant_dynamic-update-slice_fusion.4
  321.2 4.8 fusion.1
  326.0 0.6 constant_dynamic-update-slice_fusion.3
  326.6 1.6 copy-done.2
  328.2 5.0 fusion.2
  333.2 0.6 constant_dynamic-update-slice_fusion.2
  333.8 6.5 %fusion.3 = f32[1024,1024]{0,1:T(8,128)S(1)} fusion(bf16[2048,1024]{1,0:T(8,128)(2,1)S(1)} %divide_convert_fusion, bf16[2048,1024]{1,0:T(8,128)(2,1)} %collective-permute-done.2), kind=kOutput, calls=%fused_computation.12 | convolution fusion | flops 4294967296 | bytes 12582912 | tf_op jit(solution)/shard_map/dot_general | solution.py:43
  340.3 0.6 constant_dynamic-update-slice_fusion.1
  340.8 62.9 %collective-permute-done.3 = bf16[2048,1024]{1,0:T(8,128)(2,1)} collective-permute-done((bf16[2048,1024]{1,0:T(8,128)(2,1)}, bf16[2048,1024]{1,0:T(8,128)(2,1)}, u32[]{:S(2)}, u32[]{:S(2)}) %collective-permute-start.3) | collective-permute-done | bytes 4194336 | tf_op jit(solution)/shard_map/ppermute | solution.py:24
  403.7 6.5 %fusion.4 = f32[1024,1024]{0,1:T(8,128)S(1)} fusion(bf16[2048,1024]{1,0:T(8,128)(2,1)S(1)} %divide_convert_fusion, bf16[2048,1024]{1,0:T(8,128)(2,1)} %collective-permute-done.3), kind=kOutput, calls=%fused_computation.13 | convolution fusion | flops 4294967296 | bytes 12582912 | tf_op jit(solution)/shard_map/dot_general | solution.py:43
  410.2 0.6 constant_dynamic-update-slice_fusion
  410.8 7.9 %copy.7 = f32[8,2,1024,5,64]{2,4,3,0,1:T(8,128)} copy(f32[8,2,1024,5,64]{2,4,1,0,3:T(8,128)S(1)} %bitcast.23) | data formatting | bytes 41943040 | tf_op jit(solution)/shard_map/reshape | solution.py:37
  418.7 0.0 reduce-scatter.3.cloned.1.call-update
  418.7 0.0 reduce-scatter.5.cloned.1.call-start
  418.7 29.3 %reduce-scatter.3.cloned.1.call-done = f32[8,1024,5,64]{1,3,2,0:T(8,128)} async-done(((f32[16,1024,5,64]{1,3,2,0:T(8,128)}), f32[8,1024,5,64]{1,3,2,0:T(8,128)}) %reduce-scatter.3.cloned.1.call-update) | async-done | bytes 10485776 | tf_op jit(solution)/shard_map/reduce_scatter | solution.py:38
  448.1 0.0 reduce-scatter.5.cloned.1.call-update
  448.1 137.7 %reduce-scatter.5.cloned.1.call-done = f32[1,1024,5,64]{1,3,2,0:T(8,128)} async-done(((f32[8,1024,5,64]{1,3,2,0:T(8,128)}), f32[1,1024,5,64]{1,3,2,0:T(8,128)}) %reduce-scatter.5.cloned.1.call-update) | async-done | bytes 1310736 | tf_op jit(solution)/shard_map/reduce_scatter | solution.py:39
  (5 shorter events, 0.1 us)
Async XLA Ops:
  6.5 18.9 %copy-start = (f32[1024]{0:T(1024)S(1)}, f32[1024]{0:T(1024)}, u32[]{:S(2)}) copy-start(f32[1024]{0:T(1024)} %param.4) | copy-start | bytes 12292
  6.5 441.5 %reduce-scatter.3.cloned.1.call-start = ((), (), s32[]{:S(2)}) async-start(), calls=%async_computation.3 | async-start | bytes 31457280 | tf_op jit(solution)/shard_map/reduce_scatter | solution.py:38
  31.0 93.4 %collective-permute-start = (bf16[2048,1024]{1,0:T(8,128)(2,1)S(1)}, bf16[2048,1024]{1,0:T(8,128)(2,1)S(1)}, u32[]{:S(2)}, u32[]{:S(2)}) collective-permute-start(bf16[2048,1024]{1,0:T(8,128)(2,1)S(1)} %divide_convert_fusion), channel_id=1, source_target_pairs={{16,0},{32,16},{48,32},{64,48},{80,64},{96,80},{112,96},{0,112},{1... | collective-permute-start | bytes 12582920 | tf_op jit(solution)/shard_map/ppermute | solution.py:24
  124.4 93.8 %collective-permute-start.1 = (bf16[2048,1024]{1,0:T(8,128)(2,1)S(1)}, bf16[2048,1024]{1,0:T(8,128)(2,1)S(1)}, u32[]{:S(2)}, u32[]{:S(2)}) collective-permute-start(bf16[2048,1024]{1,0:T(8,128)(2,1)S(1)} %collective-permute-done), channel_id=1, source_target_pairs={{16,0},{32,16},{48,32},{64,48},{80,64},{96,80},{112,96},{0,112},{1... | collective-permute-start | bytes 12582920 | tf_op jit(solution)/shard_map/ppermute | solution.py:24
  218.2 93.0 %copy-start.1 = (bf16[2048,1024]{1,0:T(8,128)(2,1)}, bf16[2048,1024]{1,0:T(8,128)(2,1)S(1)}, u32[]{:S(2)}) copy-start(bf16[2048,1024]{1,0:T(8,128)(2,1)S(1)} %collective-permute-done.1) | copy-start | bytes 12582916
  218.2 93.0 %collective-permute-start.2 = (bf16[2048,1024]{1,0:T(8,128)(2,1)S(1)}, bf16[2048,1024]{1,0:T(8,128)(2,1)}, u32[]{:S(2)}, u32[]{:S(2)}) collective-permute-start(bf16[2048,1024]{1,0:T(8,128)(2,1)S(1)} %collective-permute-done.1), channel_id=1, source_target_pairs={{16,0},{32,16},{48,32},{64,48},{80,64},{96,80},{112,96},{0,112},{1... | collective-permute-start | bytes 12582920 | tf_op jit(solution)/shard_map/ppermute | solution.py:24
  311.2 92.6 %collective-permute-start.3 = (bf16[2048,1024]{1,0:T(8,128)(2,1)}, bf16[2048,1024]{1,0:T(8,128)(2,1)}, u32[]{:S(2)}, u32[]{:S(2)}) collective-permute-start(bf16[2048,1024]{1,0:T(8,128)(2,1)} %collective-permute-done.2), channel_id=1, source_target_pairs={{16,0},{32,16},{48,32},{64,48},{80,64},{96,80},{112,96},{0,112},{1... | collective-permute-start | bytes 12582920 | tf_op jit(solution)/shard_map/ppermute | solution.py:24
  326.0 2.2 copy-start.2
  418.7 167.2 %reduce-scatter.5.cloned.1.call-start = ((), (), s32[]{:S(2)}) async-start(), calls=%async_computation.4 | async-start | bytes 11796480 | tf_op jit(solution)/shard_map/reduce_scatter | solution.py:39
Sparse Core Ops, SparseCore 0:
  418.8 29.2 reduce-scatter.2
  452.0 133.8 reduce-scatter.4
where the time goes:
time: 593 us
  waiting for transfers between devices  498 us (84%)
  matrix products  27.4 us (5%)
  starting transfers between devices  17.2 us (3%)
  blocking collectives  15.5 us (3%)
  between operations  13.5 us (2%)
  local copies, waits for them, and re-layouts  12.4 us (2%)
  other arithmetic  8.89 us (1%)
    ppermute x4, waiting for transfers between devices, passed_along(): return lax.ppermute(block, axis, route)  331 us
    reduce_scatter x1, waiting for transfers between devices, scatter_pairs(): return lax.psum_scatter(tiles, chips, scatter_dimension=0, tiled=True)[0]  138 us
    reduce_scatter x1, waiting for transfers between devices, scatter_pairs(): tiles = lax.psum_scatter(tiles, core, scatter_dimension=0, tiled=True)  29.3 us
    dot_general x5, matrix products, product(): lax.dot_general(left, right, (((0,), (0,)), ((), ())), preferred_element_...  27.4 us
    ppermute x4, starting transfers between devices, passed_along(): return lax.ppermute(block, axis, route)  17.2 us
    all_to_all x1, blocking collectives, copy_for_each(): lax.all_to_all(jnp.broadcast_to(value[None], (peers, *value.shape)), axis...  15.5 us
  transfers between devices with their start and end apart: 6, of which 6 were waited for; matrix products, arithmetic and copies ran while one was open for 4% of the time, Pallas kernels for 0%

commit v1 on v0

v1 whole, which is shorter than its diff:
```python
import jax
import jax.numpy as jnp
from jax import lax
from jax.experimental import pallas as pl
from jax.experimental.pallas import tpu as pltpu
from jax.sharding import Mesh
from jax.sharding import PartitionSpec as P

AXES = ("x", "zl", "y", "zh", "co")
ROW = ("y", "zh", "co")
NS = 4
NT = 2

PHASES = (
    [(0, s, t) for s in range(4) for t in range(2)],
    [(1, 0, 0), (1, 0, 1)],
    [(1, 1, 0), (1, 1, 1), (3, 0, 0), (3, 1, 0)],
    [(1, 2, 0), (1, 2, 1), (3, 2, 0), (2, 0, 0), (2, 0, 1), (4, 0, 0)],
    [(1, 3, 0), (1, 3, 1), (3, 3, 0)] + [(3, s, 1) for s in range(4)] + [(4, 0, 1)],
    [(2, 1, 0), (2, 1, 1), (4, 1, 0), (4, 1, 1)],
    [(2, 2, 0), (2, 2, 1), (4, 2, 0), (4, 2, 1)],
    [(2, 3, 0), (2, 3, 1), (4, 3, 0), (4, 3, 1)],
)
ITEMS = [item for phase in PHASES for item in phase]
N = len(ITEMS)
RING = 8
CODES = [b * 8 + s * 2 + t for b, s, t in ITEMS]
WORDS = [sum(c << (6 * i) for i, c in enumerate(CODES[g:g + 5])) for g in range(0, N, 5)]


def item_of(n):
    group = n // 5
    word = sum(jnp.where(group == g, jnp.int32(w), 0) for g, w in enumerate(WORDS))
    code = lax.shift_right_logical(word, 6 * (n % 5)) % 64
    return code // 8, (code // 2) % 4, code % 2


def kernel(p_hbm, pt_hbm, out_ref, lb, rb, rel, part, d2, y1, y2, zs, z1, za,
           in_sem, xs, xr, ds, dr, y1s, y1r, y2s, y2r, z1s, z1r, zas, zar):
    x, zl, y, zh, co = (lax.axis_index(a) for a in AXES)
    xm, xp = (x + 3) % 4, (x + 1) % 4
    ym, yp, yo = (y + 3) % 4, (y + 1) % 4, (y + 2) % 4

    def remote(src, dst, send, recv, dev):
        return pltpu.make_async_remote_copy(
            src_ref=src, dst_ref=dst, send_sem=send, recv_sem=recv,
            device_id=dev, device_id_type=pl.DeviceIdType.MESH)

    loads = []
    for s in range(NS):
        loads.append(pltpu.make_async_copy(pt_hbm.at[s], rb.at[s], in_sem.at[s]))
    for t in range(NT):
        loads.append(pltpu.make_async_copy(
            p_hbm.at[:, t * 512:(t + 1) * 512], lb.at[t], in_sem.at[NS + t]))
    for c in loads:
        c.start()

    barrier = pltpu.get_barrier_semaphore()
    others = [(x, zl, y, zh, 1 - co), (x, zl, yp, zh, co), (x, zl, ym, zh, co),
              (x, zl, y, 1 - zh, co), (x, 1 - zl, y, zh, co), (x, 1 - zl, y, 1 - zh, co),
              (xm, zl, y, zh, co), (xp, zl, y, zh, co)]
    for dev in others:
        pl.semaphore_signal(barrier, inc=1, device_id=dev, device_id_type=pl.DeviceIdType.MESH)
    pl.semaphore_wait(barrier, len(others))
    for c in loads:
        c.wait()

    to_xm, to_xp, to_z = (xm, zl, y, zh, co), (xp, zl, y, zh, co), (x, 1 - zl, y, zh, co)
    flow = [remote(rb.at[s], rb.at[4 + s], xs.at[s], xr.at[s], to_xm) for s in range(4)]
    flow += [
        remote(rb.at[0], rel.at[pl.ds(0, 256)], xs.at[4], xr.at[4], to_xp),
        remote(rb.at[1], rel.at[pl.ds(256, 256)], xs.at[5], xr.at[5], to_xp),
        remote(rb.at[3, pl.ds(64, 192)], rel.at[pl.ds(512, 192)], xs.at[6], xr.at[6], to_xp),
    ]
    flow += [remote(lb.at[t], lb.at[NT + t], xs.at[7 + t], xr.at[7 + t], to_z) for t in range(NT)]
    flow += [
        remote(rb.at[6], rb.at[10], xs.at[9], xr.at[9], to_xm),
        remote(rb.at[7, pl.ds(0, 64)], rb.at[11, pl.ds(0, 64)], xs.at[10], xr.at[10], to_xm),
        remote(rel.at[pl.ds(0, 256)], rb.at[8], xs.at[11], xr.at[11], to_xp),
        remote(rel.at[pl.ds(256, 256)], rb.at[9], xs.at[12], xr.at[12], to_xp),
        remote(rel.at[pl.ds(512, 192)], rb.at[11, pl.ds(64, 192)], xs.at[13], xr.at[13], to_xp),
    ]
    for f in (0, 4, 7, 1, 5, 8, 2, 3):
        flow[f].start()

    other_half = (1 - co) * 128
    own_half = co * 128

    def d2_copy(n, slot):
        return remote(part.at[slot, pl.ds(other_half, 128)], d2.at[n], ds.at[slot], dr.at[n],
                      (x, zl, y, zh, 1 - co))

    def y1_copies(n, slot):
        base = own_half + yo * 32
        return (remote(part.at[slot, pl.ds(base, 16)], y1.at[n, 0], y1s.at[slot, 0], y1r.at[n, 0],
                       (x, zl, yp, zh, co)),
                remote(part.at[slot, pl.ds(base + 16, 16)], y1.at[n, 1], y1s.at[slot, 1],
                       y1r.at[n, 1], (x, zl, ym, zh, co)))

    def y2_copies(n, slot):
        return (remote(part.at[slot, pl.ds(own_half + yp * 32, 32)], y2.at[n, 0],
                       y2s.at[slot, 0], y2r.at[n, 0], (x, zl, yp, zh, co)),
                remote(part.at[slot, pl.ds(own_half + ym * 32, 32)], y2.at[n, 1],
                       y2s.at[slot, 1], y2r.at[n, 1], (x, zl, ym, zh, co)))

    def z1_copy(n, left):
        return remote(zs.at[n, pl.ds((1 - zh) * 16, 16)], z1.at[n], z1s.at[n], z1r.at[n],
                      (x, (zl + left) % 2, y, 1 - zh, co))

    def za_copy(n):
        return remote(zs.at[n, pl.ds(zh * 16, 16)], za.at[n], zas.at[n], zar.at[n], to_z)

    def multiply(first, count):
        @pl.loop(first, first + count)
        def _(n):
            b, s, t = item_of(n)
            left = b // 3
            right = b - 3 * left + left * (1 - zl)
            slot = n % RING
            part[slot] = jnp.dot(rb[right * 4 + s], lb[left * NT + t],
                                 preferred_element_type=jnp.float32)
            d2_copy(n, slot).start()

    def add_core(first, count):
        @pl.loop(first, first + count)
        def _(n):
            slot = n % RING
            d2_copy(n, slot).wait()
            rows = pl.ds(own_half, 128)
            part[slot, rows] = part[slot, rows] + d2[n]
            for c in y1_copies(n, slot):
                c.start()

    def add_y1(first, count):
        @pl.loop(first, first + count)
        def _(n):
            slot = n % RING
            for c in y1_copies(n, slot):
                c.wait()
            rows = pl.ds(own_half + yp * 32, 16)
            part[slot, rows] = part[slot, rows] + y1[n, 0]
            rows = pl.ds(own_half + ym * 32 + 16, 16)
            part[slot, rows] = part[slot, rows] + y1[n, 1]
            for c in y2_copies(n, slot):
                c.start()

    def add_y2(first, count):
        @pl.loop(first, first + count)
        def _(n):
            slot = n % RING
            b, _s, _t = item_of(n)
            left = b // 3
            for c in y2_copies(n, slot):
                c.wait()
            zs[n] = part[slot, pl.ds(own_half + y * 32, 32)] + y2[n, 0] + y2[n, 1]
            z1_copy(n, left).start()

            @pl.when(left == 1)
            def _():
                za_copy(n).start()

    def finish(first, count):
        @pl.loop(first, first + count)
        def _(n):
            b, s, t = item_of(n)
            left = b // 3
            z1_copy(n, left).wait()
            rows = pl.ds(pl.multiple_of(s * 16, 16), 16)
            lanes = pl.ds(pl.multiple_of(t * 512, 512), 512)

            @pl.when(left == 1)
            def _():
                za_copy(n).wait()
                out_ref[2 * (b - 3) + 1, rows, lanes] = za[n] + z1[n]

            @pl.when(left == 0)
            def _():
                out_ref[2 * b, rows, lanes] = zs[n, pl.ds(zh * 16, 16)] + z1[n]

    def arrive(*numbers):
        for f in numbers:
            flow[f].wait_recv()

    def start(*numbers):
        for f in numbers:
            flow[f].start()

    first = 0
    for number, phase in enumerate(PHASES):
        if number == 1:
            arrive(0, 4)
            start(11, 6)
        elif number == 2:
            arrive(1, 5, 7)
            start(12)
        elif number == 3:
            arrive(2)
            start(9)
            arrive(11)
        elif number == 4:
            arrive(3, 6, 8)
            start(10, 13)
        elif number == 5:
            arrive(12)
        elif number == 6:
            arrive(9)
        elif number == 7:
            arrive(10, 13)
        count = len(phase)
        multiply(first, count)
        add_core(first, count)
        add_y1(first, count)
        add_y2(first, count)
        first += count
    finish(0, N)
    for c in flow:
        c.wait_send()


def gram(panel, panel_t):
    dma = pltpu.SemaphoreType.DMA
    f32, bf16 = jnp.float32, jnp.bfloat16
    return pl.pallas_call(
        kernel,
        out_shape=jax.ShapeDtypeStruct((5, 64, 1024), f32),
        in_specs=[pl.BlockSpec(memory_space=pl.ANY)] * 2,
        out_specs=pl.BlockSpec(memory_space=pltpu.VMEM),
        scratch_shapes=[
            pltpu.VMEM((2 * NT, 2048, 512), bf16),
            pltpu.VMEM((12, 256, 2048), bf16),
            pltpu.VMEM((704, 2048), bf16),
            pltpu.VMEM((RING, 256, 512), f32),
            pltpu.VMEM((N, 128, 512), f32),
            pltpu.VMEM((N, 2, 16, 512), f32),
            pltpu.VMEM((N, 2, 32, 512), f32),
            pltpu.VMEM((N, 32, 512), f32),
            pltpu.VMEM((N, 16, 512), f32),
            pltpu.VMEM((N, 16, 512), f32),
            dma((NS + NT,)), dma((14,)), dma((14,)),
            dma((RING,)), dma((N,)),
            dma((RING, 2)), dma((N, 2)), dma((RING, 2)), dma((N, 2)),
            dma((N,)), dma((N,)), dma((N,)), dma((N,)),
        ],
        compiler_params=pltpu.CompilerParams(
            collective_id=0, has_side_effects=True, vmem_limit_bytes=67043328),
    )(panel, panel_t)


def of_everyone(value, axis):
    peers = lax.axis_size(axis)
    return lax.all_to_all(
        jnp.broadcast_to(value[None], (peers, *value.shape)), axis, 0, 0, tiled=True
    ).sum(axis=0)


def on_device(data, column_scale, keep_mask):
    values = data.astype(jnp.float32) * column_scale[None, :]
    colsq = of_everyone(jnp.sum(values * values, axis=0), ROW)
    total_rows = data.shape[0] * lax.axis_size(ROW)
    divisor = jnp.minimum(jnp.sqrt(colsq + 1.0), jnp.sqrt(jnp.float32(total_rows)))
    scaled = (keep_mask.astype(jnp.float32) * values / divisor[None, :]).astype(jnp.bfloat16)
    rows = scaled.T.reshape(4, 2, 2, 4, 16, -1).transpose(3, 2, 0, 1, 4, 5)
    band = gram(scaled, rows.reshape(4, 256, -1))
    return band.transpose(2, 0, 1)


def solution(mesh):
    split = Mesh(mesh.devices.reshape(4, 2, 4, 2, 2), AXES)
    return jax.shard_map(
        on_device,
        mesh=split,
        in_specs=(P(ROW, ("x", "zl")), P(("x", "zl")), P(ROW, ("x", "zl"))),
        out_specs=P(("x", "zl"), None, ROW),
        check_vma=False,
    )
```

time: 593 us -> 210 us (0.35)
  waiting for transfers between devices: 498 us -> 0 us
  Pallas kernels: 0 us -> 170 us
  matrix products: 27.4 us -> 0 us
  starting transfers between devices: 17.2 us -> 0 us
  between operations: 13.5 us -> 0.02 us
    ppermute x4 -> x0, waiting for transfers between devices: 331 us -> none  [passed_along(): return lax.ppermute(block, axis, route)]
    pallas_call x0 -> x1, Pallas kernels: none -> 170 us  [gram(): pl.pallas_call(kernel, out_shape=jax.ShapeDtypeStruct((5, 64, 1024), f32)...]
    reduce_scatter x2 -> x0, waiting for transfers between devices: 167 us -> none  [the longest x1 138 us: scatter_pairs(): return lax.psum_scatter(tiles, chips, scatter_dimension=0, tiled=True)[0]]
    dot_general x5 -> x0, matrix products: 27.4 us -> none  [product(): lax.dot_general(left, right, (((0,), (0,)), ((), ())), preferred_element_...]
    ppermute x4 -> x0, starting transfers between devices: 17.2 us -> none  [passed_along(): return lax.ppermute(block, axis, route)]
    transpose x0 -> x2, local copies, waits for them, and re-layouts: none -> 11.2 us  [on_device(): rows = scaled.T.reshape(4, 2, 2, 4, 16, -1).transpose(3, 2, 0, 1, 4, 5)]
    reshape x1 -> x0, local copies, waits for them, and re-layouts: 7.86 us -> none  [scatter_pairs(): tiles = tiles.reshape(*sizes, *inside).swapaxes(0, 1).reshape(-1, *inside)]
  transfers between devices with their start and end apart: 6 -> 0, of which waited for: 6 -> 0; matrix products, arithmetic and copies ran while one was open for 4% -> 0% of each run, Pallas kernels for 0% -> 0%
where the time goes in v1:
time: 210 us
  Pallas kernels  170 us (81%)
  blocking collectives  15.5 us (7%)
  local copies, waits for them, and re-layouts  13.8 us (7%)
  other arithmetic  10.3 us (5%)
    pallas_call x1, Pallas kernels, gram(): pl.pallas_call(kernel, out_shape=jax.ShapeDtypeStruct((5, 64, 1024), f32)...  170 us
    all_to_all x1, blocking collectives, of_everyone(): lax.all_to_all(jnp.broadcast_to(value[None], (peers, *value.shape)), axis...  15.5 us
    transpose x2, local copies, waits for them, and re-layouts, on_device(): rows = scaled.T.reshape(4, 2, 2, 4, 16, -1).transpose(3, 2, 0, 1, 4, 5)  11.2 us
    convert_element_type x1, other arithmetic, on_device(): (keep_mask.astype(jnp.float32) * values / divisor[None, :]).astype(jnp.bf...  6.92 us

profile of v1, /device:TPU:0, one launch (start us, length us, event | category | flops | bytes accessed | tf_op | source)
XLA Modules:
  0.0 209.9 jit_solution(17823212116334048109)
XLA Ops:
  0.0 3.3 %multiply_reduce_fusion = f32[1024]{0:T(1024)S(1)} fusion(bf16[2048,1024]{1,0:T(8,128)(2,1)} %param.3, f32[1024]{0:T(1024)} %param.4), kind=kLoop, calls=%fused_computation.1 | loop fusion | flops 8387584 | bytes 4202496 | tf_op jit(solution)/shard_map/reduce_sum | solution.py:258
  3.4 15.5 %all_to_all.6 = f32[16,1,1024]{2,1,0:T(1,128)S(1)} all-to-all(f32[16,1,1024]{2,1,0:T(1,128)S(1)} %broadcast_in_dim.2), channel_id=1, replica_groups=mesh['x'=4,'zl'=2,'y'=4,'zh'=2,'co'=2] {'y','zh','co'}, dimensions={0} | all-to-all | bytes 131072 | tf_op jit(solution)/shard_map/all_to_all | solution.py:251
  18.8 0.1 reduce_sum.19
  18.9 6.9 %divide_convert_fusion.p_hbm = bf16[2048,1024]{1,0:T(8,128)(2,1)} fusion(bf16[2048,1024]{1,0:T(8,128)(2,1)} %param.3, s32[2048,1024]{1,0:T(8,128)} %param.5, f32[1024]{0:T(1024)S(1)} %sqrt_minimum_fusion, f32[1024]{0:T(1024)} %param.4), kind=kLoop, calls=%fused_computation | loop fusion | flops 12582912 | bytes 16785408 | tf_op jit(solution)/shard_map/convert_element_type | solution.py:261
  25.8 6.5 %copy.10 = bf16[1024,2048]{1,0:T(8,128)(2,1)} copy(bf16[1024,2048]{0,1:T(8,128)(2,1)} %bitcast.6) | data formatting | bytes 8388608 | tf_op jit(solution)/shard_map/transpose | solution.py:262
  32.3 4.7 %copy.11 = bf16[4,2,4,2,16,2048]{5,4,3,2,1,0:T(8,128)(2,1)} copy(bf16[4,2,4,2,16,2048]{5,4,0,1,3,2:T(8,128)(2,1)} %bitcast.8) | data formatting | bytes 8388608 | tf_op jit(solution)/shard_map/transpose | solution.py:262
  37.0 170.3 %shard_map.37 = f32[5,64,1024]{2,1,0:T(8,128)} custom-call(bf16[2048,1024]{1,0:T(8,128)(2,1)} %divide_convert_fusion.p_hbm, bf16[4,256,2048]{2,1,0:T(8,128)(2,1)} %bitcast.7), custom_call_target="tpu_custom_call" | custom-call | tf_op jit(solution)/shard_map/pallas_call | solution.py:223
  207.3 2.5 %copy.14 = f32[1024,5,64]{0,2,1:T(8,128)} copy(f32[1024,5,64]{0,2,1:T(8,128)} %bitcast.9) | data formatting | bytes 2621440
  (2 shorter events, 0.0 us)

commit v2 on v1

--- a/solution.py
+++ b/solution.py
@@ -12,11 +12,14 @@
 NT = 2
 
 PHASES = (
-    [(0, s, t) for s in range(4) for t in range(2)],
+    [(0, 0, 0), (0, 0, 1), (0, 1, 0), (0, 1, 1)],
+    [(0, 2, 0), (0, 2, 1), (0, 3, 0), (0, 3, 1)],
     [(1, 0, 0), (1, 0, 1)],
     [(1, 1, 0), (1, 1, 1), (3, 0, 0), (3, 1, 0)],
-    [(1, 2, 0), (1, 2, 1), (3, 2, 0), (2, 0, 0), (2, 0, 1), (4, 0, 0)],
-    [(1, 3, 0), (1, 3, 1), (3, 3, 0)] + [(3, s, 1) for s in range(4)] + [(4, 0, 1)],
+    [(2, 0, 0), (2, 0, 1), (4, 0, 0)],
+    [(1, 2, 0), (1, 2, 1), (3, 2, 0)],
+    [(1, 3, 0), (1, 3, 1), (3, 3, 0), (3, 3, 1)],
+    [(3, 0, 1), (3, 1, 1), (3, 2, 1), (4, 0, 1)],
     [(2, 1, 0), (2, 1, 1), (4, 1, 0), (4, 1, 1)],
     [(2, 2, 0), (2, 2, 1), (4, 2, 0), (4, 2, 1)],
     [(2, 3, 0), (2, 3, 1), (4, 3, 0), (4, 3, 1)],
@@ -24,6 +27,7 @@
 ITEMS = [item for phase in PHASES for item in phase]
 N = len(ITEMS)
 RING = 8
+STEP = 256
 CODES = [b * 8 + s * 2 + t for b, s, t in ITEMS]
 WORDS = [sum(c << (6 * i) for i, c in enumerate(CODES[g:g + 5])) for g in range(0, N, 5)]
 
@@ -35,35 +39,98 @@
     return code // 8, (code // 2) % 4, code % 2
 
 
-def kernel(p_hbm, pt_hbm, out_ref, lb, rb, rel, part, d2, y1, y2, zs, z1, za,
-           in_sem, xs, xr, ds, dr, y1s, y1r, y2s, y2r, z1s, z1r, zas, zar):
+def kernel(data_hbm, mask_hbm, scale_ref, out_ref, lb, rb, rel, part, d2, y1, y2, zs, z1, za,
+           mask, cs, wcol, in_sem, css, csr, xs, xr, ds, dr, y1s, y1r, y2s, y2r,
+           z1s, z1r, zas, zar):
     x, zl, y, zh, co = (lax.axis_index(a) for a in AXES)
     xm, xp = (x + 3) % 4, (x + 1) % 4
     ym, yp, yo = (y + 3) % 4, (y + 1) % 4, (y + 2) % 4
+    me = y * 4 + zh * 2 + co
+    f32, bf16 = jnp.float32, jnp.bfloat16
 
     def remote(src, dst, send, recv, dev):
         return pltpu.make_async_remote_copy(
             src_ref=src, dst_ref=dst, send_sem=send, recv_sem=recv,
             device_id=dev, device_id_type=pl.DeviceIdType.MESH)
 
-    loads = []
-    for s in range(NS):
-        loads.append(pltpu.make_async_copy(pt_hbm.at[s], rb.at[s], in_sem.at[s]))
-    for t in range(NT):
-        loads.append(pltpu.make_async_copy(
-            p_hbm.at[:, t * 512:(t + 1) * 512], lb.at[t], in_sem.at[NS + t]))
-    for c in loads:
-        c.start()
+    def loads(i):
+        rows = pl.ds(pl.multiple_of(i * STEP, STEP), STEP)
+        return [pltpu.make_async_copy(mask_hbm.at[rows], mask.at[rows], in_sem.at[i, NT])] + [
+            pltpu.make_async_copy(data_hbm.at[rows, t * 512:(t + 1) * 512], lb.at[t, rows],
+                                  in_sem.at[i, t]) for t in range(NT)]
+
+    @pl.loop(0, 2048 // STEP)
+    def _(i):
+        for c in loads(i):
+            c.start()
+
+    def row_peer(r):
+        return (x, zl, r // 4, (r // 2) % 2, r % 2)
 
     barrier = pltpu.get_barrier_semaphore()
-    others = [(x, zl, y, zh, 1 - co), (x, zl, yp, zh, co), (x, zl, ym, zh, co),
-              (x, zl, y, 1 - zh, co), (x, 1 - zl, y, zh, co), (x, 1 - zl, y, 1 - zh, co),
-              (xm, zl, y, zh, co), (xp, zl, y, zh, co)]
+    others = [row_peer((me + d) % 16) for d in range(1, 16)]
+    others += [(x, 1 - zl, y, zh, co), (x, 1 - zl, y, 1 - zh, co),
+               (xm, zl, y, zh, co), (xp, zl, y, zh, co)]
     for dev in others:
         pl.semaphore_signal(barrier, inc=1, device_id=dev, device_id_type=pl.DeviceIdType.MESH)
+
+    cs[16] = jnp.zeros((8, 1024), f32)
+
+    @pl.loop(0, 2048 // STEP)
+    def _(i):
+        for c in loads(i):
+            c.wait()
+        rows = pl.ds(pl.multiple_of(i * STEP, STEP), STEP)
+        for t in range(NT):
+            lanes = slice(t * 512, (t + 1) * 512)
+            given = lb[t, rows].astype(f32)
+            values = given * scale_ref[:, lanes]
+            cs[16, :, lanes] += (values * values).reshape(STEP // 8, 8, 512).sum(axis=0)
+            kept = (given * mask[rows, lanes].astype(f32)).astype(bf16)
+            lb[t, rows] = kept
+            turned = kept.T
+            for g in range(32):
+                j = t * 32 + g
+                py, ph, pc, s = j // 16, (j // 8) % 2, (j // 4) % 2, j % 4
+                rb[s, pl.ds(pc * 128 + py * 32 + ph * 16, 16), rows] = turned[g * 16:(g + 1) * 16]
+
+    cs[me] = jnp.broadcast_to(cs[16].sum(axis=0, keepdims=True), (8, 1024))
     pl.semaphore_wait(barrier, len(others))
-    for c in loads:
-        c.wait()
+
+    def cs_copy(slot, peer):
+        return remote(cs.at[slot], cs.at[slot], css.at[peer], csr.at[slot], row_peer(peer))
+
+    @pl.loop(1, 16)
+    def _(d):
+        cs_copy(me, (me + d) % 16).start()
+
+    @pl.loop(1, 16)
+    def _(d):
+        cs_copy((me + d) % 16, (me + d) % 16).wait_recv()
+
+    colsq = cs[0]
+    for r in range(1, 16):
+        colsq = colsq + cs[r]
+    divisor = jnp.minimum(jnp.sqrt(colsq + 1.0), jnp.sqrt(jnp.float32(32768.0)))
+    weight = scale_ref[...] / divisor[0:1]
+    wcol[...] = jnp.broadcast_to(weight, (128, 1024)).T
+
+    def scale_rb(s):
+        @pl.loop(0, 16)
+        def _(r):
+            pc, py, ph = r // 8, (r // 2) % 4, r % 2
+            j = pl.multiple_of(py * 256 + ph * 128 + pc * 64 + s * 16, 16)
+            rows = pl.ds(pl.multiple_of(r * 16, 16), 16)
+            by = wcol[pl.ds(j, 16), 0:1]
+            rb[s, rows] = (rb[s, rows].astype(f32) * by).astype(bf16)
+
+    def scale_lb(t):
+        by = weight[:, t * 512:(t + 1) * 512]
+
+        @pl.loop(0, 16)
+        def _(i):
+            rows = pl.ds(pl.multiple_of(i * 128, 128), 128)
+            lb[t, rows] = (lb[t, rows].astype(f32) * by).astype(bf16)
 
     to_xm, to_xp, to_z = (xm, zl, y, zh, co), (xp, zl, y, zh, co), (x, 1 - zl, y, zh, co)
     flow = [remote(rb.at[s], rb.at[4 + s], xs.at[s], xr.at[s], to_xm) for s in range(4)]
@@ -80,8 +147,18 @@
         remote(rel.at[pl.ds(256, 256)], rb.at[9], xs.at[12], xr.at[12], to_xp),
         remote(rel.at[pl.ds(512, 192)], rb.at[11, pl.ds(64, 192)], xs.at[13], xr.at[13], to_xp),
     ]
-    for f in (0, 4, 7, 1, 5, 8, 2, 3):
-        flow[f].start()
+    scale_rb(0)
+    flow[0].start()
+    flow[4].start()
+    scale_lb(0)
+    flow[7].start()
+    scale_rb(1)
+    flow[1].start()
+    scale_lb(1)
+    flow[8].start()
+    for s in (2, 3):
+        scale_rb(s)
+        flow[s].start()
 
     other_half = (1 - co) * 128
     own_half = co * 128
@@ -185,45 +262,57 @@
         for f in numbers:
             flow[f].start()
 
-    first = 0
+    first, before = 0, None
     for number, phase in enumerate(PHASES):
-        if number == 1:
-            arrive(0, 4)
-            start(11, 6)
-        elif number == 2:
-            arrive(1, 5, 7)
-            start(12)
+        if number == 2:
+            arrive(4, 0)
+            start(11, 5)
         elif number == 3:
+            arrive(1, 7)
+        elif number == 4:
+            arrive(11)
+        elif number == 5:
+            arrive(5)
+            start(12, 6)
             arrive(2)
             start(9)
-            arrive(11)
-        elif number == 4:
-            arrive(3, 6, 8)
-            start(10, 13)
-        elif number == 5:
+        elif number == 6:
+            arrive(3, 8)
+            start(10)
+        elif number == 8:
             arrive(12)
-        elif number == 6:
+        elif number == 9:
+            arrive(6)
+            start(13)
             arrive(9)
-        elif number == 7:
+        elif number == 10:
             arrive(10, 13)
         count = len(phase)
         multiply(first, count)
         add_core(first, count)
+        if before is not None:
+            add_y2(*before)
         add_y1(first, count)
-        add_y2(first, count)
+        before = (first, count)
         first += count
+    add_y2(*before)
     finish(0, N)
     for c in flow:
         c.wait_send()
 
-
-def gram(panel, panel_t):
+    @pl.loop(1, 16)
+    def _(d):
+        cs_copy(me, (me + d) % 16).wait_send()
+
+
+def on_device(data, column_scale, keep_mask):
     dma = pltpu.SemaphoreType.DMA
     f32, bf16 = jnp.float32, jnp.bfloat16
-    return pl.pallas_call(
+    band = pl.pallas_call(
         kernel,
         out_shape=jax.ShapeDtypeStruct((5, 64, 1024), f32),
-        in_specs=[pl.BlockSpec(memory_space=pl.ANY)] * 2,
+        in_specs=[pl.BlockSpec(memory_space=pl.ANY)] * 2
+        + [pl.BlockSpec(memory_space=pltpu.VMEM)],
         out_specs=pl.BlockSpec(memory_space=pltpu.VMEM),
         scratch_shapes=[
             pltpu.VMEM((2 * NT, 2048, 512), bf16),
@@ -236,31 +325,17 @@
             pltpu.VMEM((N, 32, 512), f32),
             pltpu.VMEM((N, 16, 512), f32),
             pltpu.VMEM((N, 16, 512), f32),
-            dma((NS + NT,)), dma((14,)), dma((14,)),
+            pltpu.VMEM((2048, 1024), jnp.int32),
+            pltpu.VMEM((17, 8, 1024), f32),
+            pltpu.VMEM((1024, 128), f32),
+            dma((2048 // STEP, NT + 1)), dma((16,)), dma((16,)), dma((14,)), dma((14,)),
             dma((RING,)), dma((N,)),
             dma((RING, 2)), dma((N, 2)), dma((RING, 2)), dma((N, 2)),
             dma((N,)), dma((N,)), dma((N,)), dma((N,)),
         ],
         compiler_params=pltpu.CompilerParams(
             collective_id=0, has_side_effects=True, vmem_limit_bytes=67043328),
-    )(panel, panel_t)
-
-
-def of_everyone(value, axis):
-    peers = lax.axis_size(axis)
-    return lax.all_to_all(
-        jnp.broadcast_to(value[None], (peers, *value.shape)), axis, 0, 0, tiled=True
-    ).sum(axis=0)
-
-
-def on_device(data, column_scale, keep_mask):
-    values = data.astype(jnp.float32) * column_scale[None, :]
-    colsq = of_everyone(jnp.sum(values * values, axis=0), ROW)
-    total_rows = data.shape[0] * lax.axis_size(ROW)
-    divisor = jnp.minimum(jnp.sqrt(colsq + 1.0), jnp.sqrt(jnp.float32(total_rows)))
-    scaled = (keep_mask.astype(jnp.float32) * values / divisor[None, :]).astype(jnp.bfloat16)
-    rows = scaled.T.reshape(4, 2, 2, 4, 16, -1).transpose(3, 2, 0, 1, 4, 5)
-    band = gram(scaled, rows.reshape(4, 256, -1))
+    )(data, keep_mask, column_scale.reshape(1, 1024))
     return band.transpose(2, 0, 1)
 
 

time: 210 us -> 183 us (0.87)
  blocking collectives: 15.5 us -> 0 us
  local copies, waits for them, and re-layouts: 13.8 us -> 2.52 us
  other arithmetic: 10.3 us -> 0 us
  Pallas kernels: 170 us -> 180 us
    all_to_all x1 -> x0, blocking collectives: 15.5 us -> none  [of_everyone(): lax.all_to_all(jnp.broadcast_to(value[None], (peers, *value.shape)), axis...]
    transpose x2 -> x0, local copies, waits for them, and re-layouts: 11.2 us -> none  [on_device(): rows = scaled.T.reshape(4, 2, 2, 4, 16, -1).transpose(3, 2, 0, 1, 4, 5)]
    pallas_call x1, Pallas kernels: 170 us -> 180 us  [on_device(): pl.pallas_call(kernel, out_shape=jax.ShapeDtypeStruct((5, 64, 1024), f32)...]
    convert_element_type x1 -> x0, other arithmetic: 6.92 us -> none  [on_device(): (keep_mask.astype(jnp.float32) * values / divisor[None, :]).astype(jnp.bf...]
    reduce_sum x2 -> x0, other arithmetic: 3.39 us -> none  [the longest x1 3.34 us: on_device(): colsq = of_everyone(jnp.sum(values * values, axis=0), ROW)]
where the time goes in v2:
time: 183 us
  Pallas kernels  180 us (98%)
  local copies, waits for them, and re-layouts  2.52 us (1%)
    pallas_call x1, Pallas kernels, on_device(): pl.pallas_call(kernel, out_shape=jax.ShapeDtypeStruct((5, 64, 1024), f32)...  180 us

profile of v2, /device:TPU:0, one launch (start us, length us, event | category | flops | bytes accessed | tf_op | source)
XLA Modules:
  0.0 182.6 jit_solution(12649935483886202846)
XLA Ops:
  0.0 180.1 %shard_map.37 = f32[5,64,1024]{2,1,0:T(8,128)} custom-call(bf16[2048,1024]{1,0:T(8,128)(2,1)} %data_hbm.1, s32[2048,1024]{1,0:T(8,128)} %mask_hbm.1, f32[1,1024]{1,0:T(1,128)} %bitcast.3), custom_call_target="tpu_custom_call" | custom-call | tf_op jit(solution)/shard_map/pallas_call | solution.py:311
  180.1 2.5 %copy.5 = f32[1024,5,64]{0,2,1:T(8,128)} copy(f32[1024,5,64]{0,2,1:T(8,128)} %bitcast.2) | data formatting | bytes 2621440

commit v3 on v0

v3 whole, which is shorter than its diff:
```python
import re

import jax
import jax.numpy as jnp
from jax import lax
from jax.experimental import pallas as pl
from jax.experimental.pallas import tpu as pltpu
from jax.sharding import Mesh
from jax.sharding import PartitionSpec as P

AXES = ("x", "zl", "y", "zh", "co")
ROW = ("y", "zh", "co")
NS = 4
NT = 2

PHASES = (
    [(0, 0, 0), (0, 0, 1), (0, 1, 0), (0, 1, 1)],
    [(0, 2, 0), (0, 2, 1), (0, 3, 0), (0, 3, 1)],
    [(1, 0, 0), (1, 0, 1)],
    [(1, 1, 0), (1, 1, 1)],
    [(3, 0, 0), (3, 1, 0)],
    [(2, 0, 0), (2, 0, 1), (4, 0, 0)],
    [(1, 2, 0), (1, 2, 1), (3, 2, 0)],
    [(1, 3, 0), (1, 3, 1), (3, 3, 0)],
    [(3, 0, 1), (3, 1, 1), (3, 2, 1), (3, 3, 1)],
    [(4, 0, 1), (2, 1, 0), (2, 1, 1)],
    [(4, 1, 0), (4, 1, 1)],
    [(2, 2, 0), (2, 2, 1), (4, 2, 0), (4, 2, 1)],
    [(4, 3, 0), (4, 3, 1)],
    [(2, 3, 0), (2, 3, 1)],
)
ITEMS = [item for phase in PHASES for item in phase]
N = len(ITEMS)
RING = 16
NARROW = 9
WIDE = sum(len(phase) for phase in PHASES[:NARROW])
STEP = 256
CODES = [b * 8 + s * 2 + t for b, s, t in ITEMS]
WORDS = [sum(c << (6 * i) for i, c in enumerate(CODES[g:g + 5])) for g in range(0, N, 5)]


def item_of(n):
    group = n // 5
    word = sum(jnp.where(group == g, jnp.int32(w), 0) for g, w in enumerate(WORDS))
    code = lax.shift_right_logical(word, 6 * (n % 5)) % 64
    return code // 8, (code // 2) % 4, code % 2


def kernel(data_hbm, mask_hbm, scale_ref, out_near, out_far, lb, rb, lraw, rraw, rel, part, d2, y1, y2,
           h1, g1, h2, g2, zs, mask, acc, cs, cr, wrow, wcol, in_sem, css, csr, ws, wr, xs, xr,
           ds, dr, y1s, y1r, y2s, y2r, z1s, z1r, zas, zar):
    x, zl, y, zh, co = (lax.axis_index(a) for a in AXES)
    xm, xp = (x + 3) % 4, (x + 1) % 4
    xo = (x + 2) % 4
    ym, yp, yo = (y + 3) % 4, (y + 1) % 4, (y + 2) % 4
    f32, bf16 = jnp.float32, jnp.bfloat16

    def remote(src, dst, send, recv, dev):
        return pltpu.make_async_remote_copy(
            src_ref=src, dst_ref=dst, send_sem=send, recv_sem=recv,
            device_id=dev, device_id_type=pl.DeviceIdType.MESH)

    def load_mask(i):
        rows = pl.ds(pl.multiple_of(i * STEP, STEP), STEP)
        return pltpu.make_async_copy(mask_hbm.at[rows], mask.at[i % 3], in_sem.at[i, NT])

    def load_data(i):
        rows = pl.ds(pl.multiple_of(i * STEP, STEP), STEP)
        return [pltpu.make_async_copy(data_hbm.at[rows, t * 512:(t + 1) * 512],
                                      lraw.at[t, rows], in_sem.at[i, t]) for t in range(NT)]

    @pl.loop(0, 2048 // STEP)
    def _(i):
        for c in load_data(i):
            c.start()

        @pl.when(i < 3)
        def _():
            load_mask(i).start()

    barrier = pltpu.get_barrier_semaphore()
    others = [(x, zl, y, zh, 1 - co), (x, zl, yp, zh, co), (x, zl, ym, zh, co),
              (x, zl, y, 1 - zh, co), (x, 1 - zl, y, zh, co), (x, 1 - zl, y, 1 - zh, co),
              (xm, zl, y, zh, co), (xp, zl, y, zh, co), (xo, zl, y, zh, co)]
    for dev in others:
        pl.semaphore_signal(barrier, inc=1, device_id=dev, device_id_type=pl.DeviceIdType.MESH)

    acc[...] = jnp.zeros((8, 1024), f32)

    @pl.loop(0, 2048 // STEP)
    def _(i):
        load_mask(i).wait()
        for c in load_data(i):
            c.wait()
        rows = pl.ds(pl.multiple_of(i * STEP, STEP), STEP)
        for t in range(NT):
            lanes = slice(t * 512, (t + 1) * 512)
            given = lraw[t, rows].astype(f32)
            values = given * scale_ref[:, lanes]
            acc[:, lanes] += (values * values).reshape(STEP // 8, 8, 512).sum(axis=0)
            kept = (given * mask[i % 3, :, lanes].astype(f32)).astype(bf16)
            lraw[t, rows] = kept
            turned = kept.T
            for g in range(32):
                j = t * 32 + g
                py, ph, pc, s = j // 16, (j // 8) % 2, (j // 4) % 2, j % 4
                rraw[s, pl.ds(pc * 128 + py * 32 + ph * 16, 16), rows] = turned[g * 16:(g + 1) * 16]

        @pl.when(i + 3 < 2048 // STEP)
        def _():
            load_mask(i + 3).start()

    pl.semaphore_wait(barrier, len(others))

    to_xm, to_xp, to_z = (xm, zl, y, zh, co), (xp, zl, y, zh, co), (x, 1 - zl, y, zh, co)
    routes = {"X%d" % s: (rraw.at[s], rb.at[4 + s], to_xm) for s in range(NS)}
    pieces = ((0, 0, 128), (0, 128, 128), (1, 0, 128), (1, 128, 128), (3, 96, 80), (3, 176, 80))
    at = 0
    for i, (s, row, rows) in enumerate(pieces):
        kept, rows = pl.ds(at, rows), pl.ds(row, rows)
        at += pieces[i][2]
        routes["R%d" % i] = (rraw.at[s, rows], rel.at[kept], to_xp)
        routes["S%d" % i] = (rel.at[kept], rb.at[8 + s, rows], to_xp)
    routes["Y0"] = (rb.at[6], rb.at[10], to_xm)
    routes["Y1"] = (rb.at[7, pl.ds(0, 96)], rb.at[11, pl.ds(0, 96)], to_xm)
    for i, (t, rows) in enumerate(((0, pl.ds(0, 1024)), (0, pl.ds(1024, 1024)),
                                   (1, pl.ds(0, 1024)), (1, pl.ds(1024, 1024)))):
        routes["Z%d" % i] = (lraw.at[t, rows], lb.at[NT + t, rows], to_z)
    flow = {name: remote(src, dst, xs.at[i], xr.at[i], dev)
            for i, (name, (src, dst, dev)) in enumerate(routes.items())}

    def arrive(*names):
        for name in names:
            flow[name].wait_recv()

    def start(*names):
        for name in names:
            flow[name].start()

    start("X0", "R0", "R1")

    partners = [(x, zl, y, 1 - zh, co), (x, zl, y, zh, 1 - co),
                (x, zl, y + 1 - 2 * (y % 2), zh, co), (x, zl, 3 - y, zh, co)]
    colsq = acc[...].sum(axis=0, keepdims=True)
    sums = []
    for i, dev in enumerate(partners):
        cs[i] = colsq
        c = remote(cs.at[i], cr.at[i], css.at[i], csr.at[i], dev)
        c.start()
        c.wait_recv()
        sums.append(c)
        colsq = colsq + cr[i]
        if i == 0:
            start("Z0")
    divisor = jnp.minimum(jnp.sqrt(colsq + 1.0), jnp.sqrt(jnp.float32(32768.0)))
    wrow[0] = scale_ref[...] / divisor
    weights = [remote(wrow.at[0], wrow.at[1], ws.at[0], wr.at[0], to_xm),
               remote(wrow.at[0], wrow.at[2], ws.at[1], wr.at[1], (xo, zl, y, zh, co)),
               remote(wrow.at[0], wrow.at[3], ws.at[2], wr.at[2], to_z)]
    for w in weights:
        w.start()
    start("X1", "Z1", "Z2", "Z3", "X2", "X3")

    def turn_weights(i):
        wcol[i] = jnp.broadcast_to(wrow[i], (128, 1024)).T

    def scale_rb(src, dst, s, i, first=0):
        @pl.loop(first, 16)
        def _(r):
            pc, py, ph = r // 8, (r // 2) % 4, r % 2
            j = pl.multiple_of(py * 256 + ph * 128 + pc * 64 + s * 16, 16)
            rows = pl.ds(pl.multiple_of(r * 16, 16), 16)
            by = jnp.concatenate([wcol[i, pl.ds(j, 16)]] * 16, axis=1)
            dst[rows] = (src[rows].astype(f32) * by).astype(bf16)

    def scale_lb(src, dst, t, i):
        by = wrow[i, :, t * 512:(t + 1) * 512]

        @pl.loop(0, 16)
        def _(n):
            rows = pl.ds(pl.multiple_of(n * 128, 128), 128)
            dst[rows] = (src[rows].astype(f32) * by).astype(bf16)

    def scale_x1(s):
        scale_rb(rb.at[4 + s], rb.at[4 + s], s, 1)

    def scale_x2(s, first=0):
        scale_rb(rb.at[8 + s], rb.at[8 + s], s, 2, first)

    def scale_z(t):
        scale_lb(lb.at[NT + t], lb.at[NT + t], t, 3)

    other_half = (1 - co) * 128
    own_half = co * 128

    def d2_copy(n, slot):
        return remote(part.at[slot, pl.ds(other_half, 128)], d2.at[slot], ds.at[slot], dr.at[slot],
                      (x, zl, y, zh, 1 - co))

    far = (own_half + yo * 32, own_half + yo * 32 + 16)
    near = (own_half + yp * 32, own_half + ym * 32)
    via = (own_half + yp * 32, own_half + ym * 32 + 16)
    neighbours = ((x, zl, yp, zh, co), (x, zl, ym, zh, co))

    def y1_copies(n, slot, narrow):
        return [remote(h1.at[slot, d] if narrow else part.at[slot, pl.ds(far[d], 16)],
                       g1.at[n - WIDE, d] if narrow else y1.at[n, d],
                       y1s.at[slot, d], y1r.at[n, d], neighbours[d]) for d in range(2)]

    def y2_copies(n, slot, narrow):
        return [remote(h2.at[slot, d] if narrow else part.at[slot, pl.ds(near[d], 32)],
                       g2.at[n - WIDE, d] if narrow else y2.at[n, d],
                       y2s.at[slot, d], y2r.at[n, d], neighbours[d]) for d in range(2)]

    def place(out, b, s, t):
        left = b // 3
        k = 2 * (b - 3 * left) + left
        return out.at[k, pl.ds(pl.multiple_of(s * 16, 16), 16),
                      pl.ds(pl.multiple_of(t * 512, 512), 512)]

    def z1_copy(n, item):
        return remote(zs.at[n, pl.ds((1 - zh) * 16, 16)], place(out_far, *item), z1s.at[n],
                      z1r.at[n], (x, (zl + item[0] // 3) % 2, y, 1 - zh, co))

    def za_copy(n, item):
        return remote(zs.at[n, pl.ds(zh * 16, 16)], place(out_near, *item), zas.at[n],
                      zar.at[n], to_z)

    def multiply(first, count, _narrow):
        @pl.loop(first, first + count)
        def _(n):
            b, s, t = item_of(n)
            left = b // 3
            right = b - 3 * left + left * (1 - zl)
            slot = n % RING
            part[slot] = jnp.dot(rb[right * 4 + s], lb[left * NT + t],
                                 preferred_element_type=jnp.float32)
            d2_copy(n, slot).start()

    def add_core(first, count, narrow):
        @pl.loop(first, first + count)
        def _(n):
            slot = n % RING
            d2_copy(n, slot).wait()
            rows = pl.ds(own_half, 128)
            part[slot, rows] = part[slot, rows] + d2[slot]
            for d, c in enumerate(y1_copies(n, slot, narrow)):
                if narrow:
                    h1[slot, d] = part[slot, pl.ds(far[d], 16)].astype(bf16)
                c.start()

    def add_y1(first, count, narrow):
        @pl.loop(first, first + count)
        def _(n):
            slot = n % RING
            for c in y1_copies(n, slot, narrow):
                c.wait()
            for d in range(2):
                rows = pl.ds(via[d], 16)
                came = g1[n - WIDE, d].astype(f32) if narrow else y1[n, d]
                part[slot, rows] = part[slot, rows] + came
            for d, c in enumerate(y2_copies(n, slot, narrow)):
                if narrow:
                    h2[slot, d] = part[slot, pl.ds(near[d], 32)].astype(bf16)
                c.start()

    def add_y2(first, count, narrow):
        @pl.loop(first, first + count)
        def _(n):
            slot = n % RING
            item = item_of(n)
            left = item[0] // 3
            for c in y2_copies(n, slot, narrow):
                c.wait()
            total = part[slot, pl.ds(own_half + y * 32, 32)]
            for d in range(2):
                total = total + (g2[n - WIDE, d].astype(f32) if narrow else y2[n, d])
            zs[n] = total
            z1_copy(n, item).start()

            @pl.when(left == 1)
            def _():
                za_copy(n, item).start()

            @pl.when(left == 0)
            def _():
                place(out_near, *item)[...] = zs[n, pl.ds(zh * 16, 16)]

    firsts = [sum(len(p) for p in PHASES[:g]) for g in range(len(PHASES))]

    def stages(text):
        for word in re.findall("[CDEF][0-9]+", text):
            stage = {"C": multiply, "D": add_core, "E": add_y1, "F": add_y2}[word[0]]
            g = int(word[1:])
            stage(firsts[g], len(PHASES[g]), g >= NARROW)

    turn_weights(0)
    for t in range(NT):
        scale_lb(lraw.at[t], lb.at[t], t, 0)
    scale_rb(rraw.at[0], rb.at[0], 0, 0)
    scale_rb(rraw.at[1], rb.at[1], 1, 0)
    stages("C0D0")
    arrive("R0")
    start("S0", "R2")
    scale_rb(rraw.at[2], rb.at[2], 2, 0)
    scale_rb(rraw.at[3], rb.at[3], 3, 0)
    stages("C1D1E0")
    arrive("R1")
    start("S1", "R3")
    arrive("X0")
    weights[0].wait_recv()
    turn_weights(1)
    scale_x1(0)
    stages("C2D2E1F0E2F1F2")
    arrive("X1")
    scale_x1(1)
    stages("C3D3")
    weights[2].wait_recv()
    arrive("R2")
    start("S2", "R4")
    arrive("Z0", "Z1")
    scale_z(0)
    stages("C4D4E3")
    weights[1].wait_recv()
    turn_weights(2)
    arrive("S0", "S1")
    scale_x2(0)
    stages("C5D5E4F3E5F4F5")
    arrive("R3")
    start("S3", "R5")
    arrive("X2")
    scale_x1(2)
    start("Y0")
    stages("C6D6E6F6")
    arrive("R4")
    start("S4")
    arrive("X3")
    scale_x1(3)
    start("Y1")
    stages("C7D7")
    arrive("Z2", "Z3")
    scale_z(1)
    stages("C8E7D8")
    arrive("S2", "S3")
    scale_x2(1)
    stages("C9D9C10D10")
    arrive("R5")
    start("S5")
    stages("E8E9E10F7")
    arrive("Y0")
    stages("C11D11F8F9F10E11")
    arrive("Y1", "S4", "S5")
    scale_x2(3, 6)
    stages("C12C13D12D13F11E12E13")
    stages("F12F13")
    for n, item in enumerate(ITEMS):
        z1_copy(n, item).wait()
        if item[0] >= 3:
            za_copy(n, item).wait()
    for c in list(flow.values()) + sums + weights:
        c.wait_send()


def on_device(data, column_scale, keep_mask):
    dma = pltpu.SemaphoreType.DMA
    f32, bf16 = jnp.float32, jnp.bfloat16
    near, far = pl.pallas_call(
        kernel,
        out_shape=[pltpu.VMEM((5, 64, 1024), f32)] * 2,
        in_specs=[pl.BlockSpec(memory_space=pl.ANY)] * 2
        + [pl.BlockSpec(memory_space=pltpu.VMEM)],
        out_specs=[pl.BlockSpec(memory_space=pltpu.VMEM)] * 2,
        scratch_shapes=[
            pltpu.VMEM((2 * NT, 2048, 512), bf16),
            pltpu.VMEM((12, 256, 2048), bf16),
            pltpu.VMEM((NT, 2048, 512), bf16),
            pltpu.VMEM((NS, 256, 2048), bf16),
            pltpu.VMEM((672, 2048), bf16),
            pltpu.VMEM((RING, 256, 512), f32),
            pltpu.VMEM((RING, 128, 512), f32),
            pltpu.VMEM((WIDE, 2, 16, 512), f32),
            pltpu.VMEM((WIDE, 2, 32, 512), f32),
            pltpu.VMEM((RING, 2, 16, 512), bf16),
            pltpu.VMEM((N - WIDE, 2, 16, 512), bf16),
            pltpu.VMEM((RING, 2, 32, 512), bf16),
            pltpu.VMEM((N - WIDE, 2, 32, 512), bf16),
            pltpu.VMEM((N, 32, 512), f32),
            pltpu.VMEM((3, STEP, 1024), jnp.int32),
            pltpu.VMEM((8, 1024), f32),
            pltpu.VMEM((4, 1, 1024), f32),
            pltpu.VMEM((4, 1, 1024), f32),
            pltpu.VMEM((4, 1, 1024), f32),
            pltpu.VMEM((3, 1024, 128), f32),
            dma((2048 // STEP, NT + 1)), dma((4,)), dma((4,)), dma((3,)), dma((3,)),
            dma((22,)), dma((22,)), dma((RING,)), dma((RING,)),
            dma((RING, 2)), dma((N, 2)), dma((RING, 2)), dma((N, 2)),
            dma((N,)), dma((N,)), dma((N,)), dma((N,)),
        ],
        compiler_params=pltpu.CompilerParams(
            collective_id=0, has_side_effects=True, vmem_limit_bytes=61 * 2**20),
    )(data, keep_mask, column_scale.reshape(1, 1024))
    return (near + far).transpose(2, 0, 1)


def solution(mesh):
    split = Mesh(mesh.devices.reshape(4, 2, 4, 2, 2), AXES)
    return jax.shard_map(
        on_device,
        mesh=split,
        in_specs=(P(ROW, ("x", "zl")), P(("x", "zl")), P(ROW, ("x", "zl"))),
        out_specs=P(("x", "zl"), None, ROW),
        check_vma=False,
    )
```

time: 593 us -> 155 us (0.26)
  waiting for transfers between devices: 498 us -> 0 us
  Pallas kernels: 0 us -> 153 us
  matrix products: 27.4 us -> 0 us
  starting transfers between devices: 17.2 us -> 0 us
  blocking collectives: 15.5 us -> 0 us
  between operations: 13.5 us -> 0.01 us
  local copies, waits for them, and re-layouts: 12.4 us -> 0 us
  other arithmetic: 8.89 us -> 1.32 us
    ppermute x4 -> x0, waiting for transfers between devices: 331 us -> none  [passed_along(): return lax.ppermute(block, axis, route)]
    reduce_scatter x2 -> x0, waiting for transfers between devices: 167 us -> none  [the longest x1 138 us: scatter_pairs(): return lax.psum_scatter(tiles, chips, scatter_dimension=0, tiled=True)[0]]
    pallas_call x0 -> x1, Pallas kernels: none -> 153 us  [on_device(): pl.pallas_call(kernel, out_shape=[pltpu.VMEM((5, 64, 1024), f32)] * 2, in...]
    dot_general x5 -> x0, matrix products: 27.4 us -> none  [product(): lax.dot_general(left, right, (((0,), (0,)), ((), ())), preferred_element_...]
    ppermute x4 -> x0, starting transfers between devices: 17.2 us -> none  [passed_along(): return lax.ppermute(block, axis, route)]
    all_to_all x1 -> x0, blocking collectives: 15.5 us -> none  [copy_for_each(): lax.all_to_all(jnp.broadcast_to(value[None], (peers, *value.shape)), axis...]
    reshape x1 -> x0, local copies, waits for them, and re-layouts: 7.86 us -> none  [scatter_pairs(): tiles = tiles.reshape(*sizes, *inside).swapaxes(0, 1).reshape(-1, *inside)]
  transfers between devices with their start and end apart: 6 -> 0, of which waited for: 6 -> 0; matrix products, arithmetic and copies ran while one was open for 4% -> 0% of each run, Pallas kernels for 0% -> 0%
where the time goes in v3:
time: 155 us; the launch traced here: 154 us
  Pallas kernels  153 us (99%)
    pallas_call x1, Pallas kernels, on_device(): pl.pallas_call(kernel, out_shape=[pltpu.VMEM((5, 64, 1024), f32)] * 2, in...  153 us

profile of v3, /device:TPU:0, one launch (start us, length us, event | category | flops | bytes accessed | tf_op | source)
XLA Modules:
  0.0 154.4 jit_solution(6805554676446152709)
XLA Ops:
  0.0 153.1 %shard_map.37 = (f32[5,64,1024]{2,1,0:T(8,128)S(1)}, f32[5,64,1024]{2,1,0:T(8,128)S(1)}) custom-call(bf16[2048,1024]{1,0:T(8,128)(2,1)} %data_hbm.1, s32[2048,1024]{1,0:T(8,128)} %mask_hbm.1, f32[1,1024]{1,0:T(1,128)} %bitcast.3), custom_call_target="tpu_custom_call" | custom-call | tf_op jit(solution)/shard_map/pallas_call | solution.py:367
  153.1 1.3 add_bitcast_fusion

commit v4 on v3

--- a/solution.py
+++ b/solution.py
@@ -35,6 +35,7 @@
 NARROW = 9
 WIDE = sum(len(phase) for phase in PHASES[:NARROW])
 STEP = 256
+MASKS = 6
 CODES = [b * 8 + s * 2 + t for b, s, t in ITEMS]
 WORDS = [sum(c << (6 * i) for i, c in enumerate(CODES[g:g + 5])) for g in range(0, N, 5)]
 
@@ -48,7 +49,7 @@
 
 def kernel(data_hbm, mask_hbm, scale_ref, out_near, out_far, lb, rb, lraw, rraw, rel, part, d2, y1, y2,
            h1, g1, h2, g2, zs, mask, acc, cs, cr, wrow, wcol, in_sem, css, csr, ws, wr, xs, xr,
-           ds, dr, y1s, y1r, y2s, y2r, z1s, z1r, zas, zar):
+           ds, dr, y1s, y1r, y2s, y2r, zsem):
     x, zl, y, zh, co = (lax.axis_index(a) for a in AXES)
     xm, xp = (x + 3) % 4, (x + 1) % 4
     xo = (x + 2) % 4
@@ -62,7 +63,7 @@
 
     def load_mask(i):
         rows = pl.ds(pl.multiple_of(i * STEP, STEP), STEP)
-        return pltpu.make_async_copy(mask_hbm.at[rows], mask.at[i % 3], in_sem.at[i, NT])
+        return pltpu.make_async_copy(mask_hbm.at[rows], mask.at[i % MASKS], in_sem.at[i, NT])
 
     def load_data(i):
         rows = pl.ds(pl.multiple_of(i * STEP, STEP), STEP)
@@ -74,7 +75,7 @@
         for c in load_data(i):
             c.start()
 
-        @pl.when(i < 3)
+        @pl.when(i < MASKS)
         def _():
             load_mask(i).start()
 
@@ -87,8 +88,7 @@
 
     acc[...] = jnp.zeros((8, 1024), f32)
 
-    @pl.loop(0, 2048 // STEP)
-    def _(i):
+    def take(i):
         load_mask(i).wait()
         for c in load_data(i):
             c.wait()
@@ -98,7 +98,7 @@
             given = lraw[t, rows].astype(f32)
             values = given * scale_ref[:, lanes]
             acc[:, lanes] += (values * values).reshape(STEP // 8, 8, 512).sum(axis=0)
-            kept = (given * mask[i % 3, :, lanes].astype(f32)).astype(bf16)
+            kept = (given * mask[i % MASKS, :, lanes].astype(f32)).astype(bf16)
             lraw[t, rows] = kept
             turned = kept.T
             for g in range(32):
@@ -106,20 +106,26 @@
                 py, ph, pc, s = j // 16, (j // 8) % 2, (j // 4) % 2, j % 4
                 rraw[s, pl.ds(pc * 128 + py * 32 + ph * 16, 16), rows] = turned[g * 16:(g + 1) * 16]
 
-        @pl.when(i + 3 < 2048 // STEP)
+        @pl.when(i + MASKS < 2048 // STEP)
         def _():
-            load_mask(i + 3).start()
-
+            load_mask(i + MASKS).start()
+
+    pl.loop(0, 1024 // STEP)(take)
     pl.semaphore_wait(barrier, len(others))
 
     to_xm, to_xp, to_z = (xm, zl, y, zh, co), (xp, zl, y, zh, co), (x, 1 - zl, y, zh, co)
-    routes = {"X%d" % s: (rraw.at[s], rb.at[4 + s], to_xm) for s in range(NS)}
+    routes = {"X%d" % s: (rraw.at[s], rb.at[4 + s], to_xm) for s in range(1, NS)}
+    for i, lanes in enumerate((pl.ds(0, 1024), pl.ds(1024, 1024))):
+        routes["X%d" % (4 * i)] = (rraw.at[0, :, lanes], rb.at[4, :, lanes], to_xm)
+        rows = pl.ds(0, 128)
+        routes["R%d" % (6 * i)] = (rraw.at[0, rows, lanes], rel.at[rows, lanes], to_xp)
     pieces = ((0, 0, 128), (0, 128, 128), (1, 0, 128), (1, 128, 128), (3, 96, 80), (3, 176, 80))
     at = 0
     for i, (s, row, rows) in enumerate(pieces):
         kept, rows = pl.ds(at, rows), pl.ds(row, rows)
         at += pieces[i][2]
-        routes["R%d" % i] = (rraw.at[s, rows], rel.at[kept], to_xp)
+        if i > 0:
+            routes["R%d" % i] = (rraw.at[s, rows], rel.at[kept], to_xp)
         routes["S%d" % i] = (rel.at[kept], rb.at[8 + s, rows], to_xp)
     routes["Y0"] = (rb.at[6], rb.at[10], to_xm)
     routes["Y1"] = (rb.at[7, pl.ds(0, 96)], rb.at[11, pl.ds(0, 96)], to_xm)
@@ -137,7 +143,9 @@
         for name in names:
             flow[name].start()
 
-    start("X0", "R0", "R1")
+    start("X0", "R0")
+    pl.loop(1024 // STEP, 2048 // STEP)(take)
+    start("X4", "R6", "R1")
 
     partners = [(x, zl, y, 1 - zh, co), (x, zl, y, zh, 1 - co),
                 (x, zl, y + 1 - 2 * (y % 2), zh, co), (x, zl, 3 - y, zh, co)]
@@ -204,13 +212,13 @@
 
     def y1_copies(n, slot, narrow):
         return [remote(h1.at[slot, d] if narrow else part.at[slot, pl.ds(far[d], 16)],
-                       g1.at[n - WIDE, d] if narrow else y1.at[n, d],
-                       y1s.at[slot, d], y1r.at[n, d], neighbours[d]) for d in range(2)]
+                       g1.at[n - WIDE, d] if narrow else y1.at[slot, d],
+                       y1s.at[slot, d], y1r.at[slot, d], neighbours[d]) for d in range(2)]
 
     def y2_copies(n, slot, narrow):
         return [remote(h2.at[slot, d] if narrow else part.at[slot, pl.ds(near[d], 32)],
-                       g2.at[n - WIDE, d] if narrow else y2.at[n, d],
-                       y2s.at[slot, d], y2r.at[n, d], neighbours[d]) for d in range(2)]
+                       g2.at[n - WIDE, d] if narrow else y2.at[slot, d],
+                       y2s.at[slot, d], y2r.at[slot, d], neighbours[d]) for d in range(2)]
 
     def place(out, b, s, t):
         left = b // 3
@@ -219,12 +227,12 @@
                       pl.ds(pl.multiple_of(t * 512, 512), 512)]
 
     def z1_copy(n, item):
-        return remote(zs.at[n, pl.ds((1 - zh) * 16, 16)], place(out_far, *item), z1s.at[n],
-                      z1r.at[n], (x, (zl + item[0] // 3) % 2, y, 1 - zh, co))
+        return remote(zs.at[n, pl.ds((1 - zh) * 16, 16)], place(out_far, *item), zsem.at[0],
+                      zsem.at[1], (x, (zl + item[0] // 3) % 2, y, 1 - zh, co))
 
     def za_copy(n, item):
-        return remote(zs.at[n, pl.ds(zh * 16, 16)], place(out_near, *item), zas.at[n],
-                      zar.at[n], to_z)
+        return remote(zs.at[n, pl.ds(zh * 16, 16)], place(out_near, *item), zsem.at[2],
+                      zsem.at[3], to_z)
 
     def multiply(first, count, _narrow):
         @pl.loop(first, first + count)
@@ -257,7 +265,7 @@
                 c.wait()
             for d in range(2):
                 rows = pl.ds(via[d], 16)
-                came = g1[n - WIDE, d].astype(f32) if narrow else y1[n, d]
+                came = g1[n - WIDE, d].astype(f32) if narrow else y1[slot, d]
                 part[slot, rows] = part[slot, rows] + came
             for d, c in enumerate(y2_copies(n, slot, narrow)):
                 if narrow:
@@ -274,7 +282,7 @@
                 c.wait()
             total = part[slot, pl.ds(own_half + y * 32, 32)]
             for d in range(2):
-                total = total + (g2[n - WIDE, d].astype(f32) if narrow else y2[n, d])
+                total = total + (g2[n - WIDE, d].astype(f32) if narrow else y2[slot, d])
             zs[n] = total
             z1_copy(n, item).start()
 
@@ -300,14 +308,14 @@
     scale_rb(rraw.at[0], rb.at[0], 0, 0)
     scale_rb(rraw.at[1], rb.at[1], 1, 0)
     stages("C0D0")
-    arrive("R0")
+    arrive("R0", "R6")
     start("S0", "R2")
     scale_rb(rraw.at[2], rb.at[2], 2, 0)
     scale_rb(rraw.at[3], rb.at[3], 3, 0)
     stages("C1D1E0")
     arrive("R1")
     start("S1", "R3")
-    arrive("X0")
+    arrive("X0", "X4")
     weights[0].wait_recv()
     turn_weights(1)
     scale_x1(0)
@@ -353,10 +361,9 @@
     scale_x2(3, 6)
     stages("C12C13D12D13F11E12E13")
     stages("F12F13")
-    for n, item in enumerate(ITEMS):
-        z1_copy(n, item).wait()
-        if item[0] >= 3:
-            za_copy(n, item).wait()
+    remote(out_far, out_far, zsem.at[0], zsem.at[1], to_z).wait()
+    some = out_near.at[pl.ds(0, 2)]
+    remote(some, some, zsem.at[2], zsem.at[3], to_z).wait()
     for c in list(flow.values()) + sums + weights:
         c.wait_send()
 
@@ -378,23 +385,22 @@
             pltpu.VMEM((672, 2048), bf16),
             pltpu.VMEM((RING, 256, 512), f32),
             pltpu.VMEM((RING, 128, 512), f32),
-            pltpu.VMEM((WIDE, 2, 16, 512), f32),
-            pltpu.VMEM((WIDE, 2, 32, 512), f32),
+            pltpu.VMEM((RING, 2, 16, 512), f32),
+            pltpu.VMEM((RING, 2, 32, 512), f32),
             pltpu.VMEM((RING, 2, 16, 512), bf16),
             pltpu.VMEM((N - WIDE, 2, 16, 512), bf16),
             pltpu.VMEM((RING, 2, 32, 512), bf16),
             pltpu.VMEM((N - WIDE, 2, 32, 512), bf16),
             pltpu.VMEM((N, 32, 512), f32),
-            pltpu.VMEM((3, STEP, 1024), jnp.int32),
+            pltpu.VMEM((MASKS, STEP, 1024), jnp.int32),
             pltpu.VMEM((8, 1024), f32),
             pltpu.VMEM((4, 1, 1024), f32),
             pltpu.VMEM((4, 1, 1024), f32),
             pltpu.VMEM((4, 1, 1024), f32),
             pltpu.VMEM((3, 1024, 128), f32),
             dma((2048 // STEP, NT + 1)), dma((4,)), dma((4,)), dma((3,)), dma((3,)),
-            dma((22,)), dma((22,)), dma((RING,)), dma((RING,)),
-            dma((RING, 2)), dma((N, 2)), dma((RING, 2)), dma((N, 2)),
-            dma((N,)), dma((N,)), dma((N,)), dma((N,)),
+            dma((24,)), dma((24,)), dma((RING,)), dma((RING,)),
+            dma((RING, 2)), dma((RING, 2)), dma((RING, 2)), dma((RING, 2)), dma((4,)),
         ],
         compiler_params=pltpu.CompilerParams(
             collective_id=0, has_side_effects=True, vmem_limit_bytes=61 * 2**20),

time: 155 us -> 150 us (0.968)
  Pallas kernels: 153 us -> 148 us
    pallas_call x1, Pallas kernels: 153 us -> 148 us  [on_device(): pl.pallas_call(kernel, out_shape=[pltpu.VMEM((5, 64, 1024), f32)] * 2, in...]
where the time goes in v4:
time: 150 us; the launch traced here: 149 us
  Pallas kernels  148 us (99%)
    pallas_call x1, Pallas kernels, on_device(): pl.pallas_call(kernel, out_shape=[pltpu.VMEM((5, 64, 1024), f32)] * 2, in...  148 us

profile of v4, /device:TPU:0, one launch (start us, length us, event | category | flops | bytes accessed | tf_op | source)
XLA Modules:
  0.0 149.5 jit_solution(15552212709825101862)
XLA Ops:
  0.0 148.1 %shard_map.37 = (f32[5,64,1024]{2,1,0:T(8,128)S(1)}, f32[5,64,1024]{2,1,0:T(8,128)S(1)}) custom-call(bf16[2048,1024]{1,0:T(8,128)(2,1)} %data_hbm.1, s32[2048,1024]{1,0:T(8,128)} %mask_hbm.1, f32[1,1024]{1,0:T(1,128)} %bitcast.3), custom_call_target="tpu_custom_call" | custom-call | tf_op jit(solution)/shard_map/pallas_call | solution.py:374
  148.2 1.3 add_bitcast_fusion

commit v5 on v4

--- a/solution.py
+++ b/solution.py
@@ -70,21 +70,21 @@
         return [pltpu.make_async_copy(data_hbm.at[rows, t * 512:(t + 1) * 512],
                                       lraw.at[t, rows], in_sem.at[i, t]) for t in range(NT)]
 
-    @pl.loop(0, 2048 // STEP)
-    def _(i):
-        for c in load_data(i):
-            c.start()
-
-        @pl.when(i < MASKS)
-        def _():
-            load_mask(i).start()
-
     barrier = pltpu.get_barrier_semaphore()
     others = [(x, zl, y, zh, 1 - co), (x, zl, yp, zh, co), (x, zl, ym, zh, co),
               (x, zl, y, 1 - zh, co), (x, 1 - zl, y, zh, co), (x, 1 - zl, y, 1 - zh, co),
               (xm, zl, y, zh, co), (xp, zl, y, zh, co), (xo, zl, y, zh, co)]
     for dev in others:
         pl.semaphore_signal(barrier, inc=1, device_id=dev, device_id_type=pl.DeviceIdType.MESH)
+
+    @pl.loop(0, 2048 // STEP)
+    def _(i):
+        for c in load_data(i):
+            c.start()
+
+        @pl.when(i < MASKS)
+        def _():
+            load_mask(i).start()
 
     acc[...] = jnp.zeros((8, 1024), f32)
 
@@ -129,8 +129,9 @@
         routes["S%d" % i] = (rel.at[kept], rb.at[8 + s, rows], to_xp)
     routes["Y0"] = (rb.at[6], rb.at[10], to_xm)
     routes["Y1"] = (rb.at[7, pl.ds(0, 96)], rb.at[11, pl.ds(0, 96)], to_xm)
-    for i, (t, rows) in enumerate(((0, pl.ds(0, 1024)), (0, pl.ds(1024, 1024)),
-                                   (1, pl.ds(0, 1024)), (1, pl.ds(1024, 1024)))):
+    for i, (t, rows) in enumerate(((0, pl.ds(256, 768)), (0, pl.ds(1024, 1024)),
+                                   (1, pl.ds(0, 1024)), (1, pl.ds(1024, 1024)),
+                                   (0, pl.ds(0, 256)))):
         routes["Z%d" % i] = (lraw.at[t, rows], lb.at[NT + t, rows], to_z)
     flow = {name: remote(src, dst, xs.at[i], xr.at[i], dev)
             for i, (name, (src, dst, dev)) in enumerate(routes.items())}
@@ -143,7 +144,7 @@
         for name in names:
             flow[name].start()
 
-    start("X0", "R0")
+    start("X0", "R0", "Z4")
     pl.loop(1024 // STEP, 2048 // STEP)(take)
     start("X4", "R6", "R1")
 
@@ -326,7 +327,7 @@
     weights[2].wait_recv()
     arrive("R2")
     start("S2", "R4")
-    arrive("Z0", "Z1")
+    arrive("Z0", "Z1", "Z4")
     scale_z(0)
     stages("C4D4E3")
     weights[1].wait_recv()
@@ -399,7 +400,7 @@
             pltpu.VMEM((4, 1, 1024), f32),
             pltpu.VMEM((3, 1024, 128), f32),
             dma((2048 // STEP, NT + 1)), dma((4,)), dma((4,)), dma((3,)), dma((3,)),
-            dma((24,)), dma((24,)), dma((RING,)), dma((RING,)),
+            dma((25,)), dma((25,)), dma((RING,)), dma((RING,)),
             dma((RING, 2)), dma((RING, 2)), dma((RING, 2)), dma((RING, 2)), dma((4,)),
         ],
         compiler_params=pltpu.CompilerParams(

time: 150 us -> 150 us (level)
  no operation moved by 1% of the time
where the time goes in v5:
time: 150 us; the launch traced here: 149 us
  Pallas kernels  148 us (99%)
    pallas_call x1, Pallas kernels, on_device(): pl.pallas_call(kernel, out_shape=[pltpu.VMEM((5, 64, 1024), f32)] * 2, in...  148 us

profile of v5, /device:TPU:0, one launch (start us, length us, event | category | flops | bytes accessed | tf_op | source)
XLA Modules:
  0.0 149.5 jit_solution(16932450223688975713)
XLA Ops:
  0.0 148.2 %shard_map.37 = (f32[5,64,1024]{2,1,0:T(8,128)S(1)}, f32[5,64,1024]{2,1,0:T(8,128)S(1)}) custom-call(bf16[2048,1024]{1,0:T(8,128)(2,1)} %data_hbm.1, s32[2048,1024]{1,0:T(8,128)} %mask_hbm.1, f32[1,1024]{1,0:T(1,128)} %bitcast.3), custom_call_target="tpu_custom_call" | custom-call | tf_op jit(solution)/shard_map/pallas_call | solution.py:375
  148.2 1.3 add_bitcast_fusion
